TPU v7x, 32 devices: a whole 2x2x4 slice. The times are simulated.
32 devices in a mesh: grp: 4 (over y, x), dev: 8 (over z, core).
Axes of the slice: x: 2, y: 2, z: 4, core: 2. Of those that a mesh axis runs over, the one named last changes fastest.
Arguments:
- acts: bfloat16 [8192, 12288], P(('grp', 'dev')), may hold values from -6 to 6
- grads_out: bfloat16 [8192, 64], P(('grp', 'dev')), may hold values from -0.375 to 0.375
- residual_in: float32 [32, 64, 12288], P(('grp', 'dev')), may hold values from -6 to 6
- sel_index: int32 [32, 64], P(('grp', 'dev')), may hold values from 0 to 6143, as said below
- sel_count: int32 [32], P(('grp', 'dev')), may hold values from 16 to 64, as said below
- momentum_in: float32 [64, 12288], P(None, 'dev'), may hold values from -6 to 6
Outputs:
- residual_out: float32 [32, 64, 12288], P(('grp', 'dev'))
- momentum_out: float32 [64, 12288], P(None, 'dev')
Inputs may be any that keep to these rules, and one draw needn't show every extreme that they name: `sel_index`: the 64 numbers of a row are distinct. `sel_count`: equal to 64 on some device in every draw.
All inputs are finite; a program needn't handle non-finite values.
Results may differ from a plain program's by a relative error of at most 0.0003.
Values sent between devices are 32-bit elements; how exact they have to be, the bound alone decides.
A program may use at most 64 MiB of HBM per device.

v0:
```python
import jax
import jax.numpy as jnp
from jax import lax
from jax.sharding import PartitionSpec as P

momentum_decay = 0.9


def from_behind(block, axis, distance):
    devices = range(lax.axis_size(axis))
    route = [((i - distance) % len(devices), i) for i in devices]
    return lax.ppermute(block, axis, route)


def local(acts, grads_out, residual_in, sel_index, sel_count, momentum_in):
    width = acts.shape[1]
    columns = grads_out.shape[1]
    slots = sel_index.shape[1]
    n_blocks = columns * width // 128
    part_width = momentum_in.shape[1]
    local_grad = lax.dot_general(
        grads_out, acts, (((0,), (0,)), ((), ())), preferred_element_type=jnp.float32
    )
    summed = residual_in[0] + local_grad
    blocks = summed.reshape(n_blocks, 128)
    chosen = sel_index[0]
    valid_rows = (jnp.arange(slots, dtype=jnp.int32) < sel_count[0]).astype(jnp.float32)
    picked = blocks[chosen] * valid_rows[:, None]
    marked = jnp.zeros((n_blocks,), jnp.float32).at[chosen].max(valid_rows)
    kept = (blocks * (1.0 - marked)[:, None]).reshape(1, columns, width)
    labels = chosen.astype(jnp.float32)
    group_vals, group_labels = (
        lax.all_gather(picked, "dev", axis=0, tiled=True),
        lax.all_gather(labels, "dev", axis=0, tiled=True),
    )
    n_groups = lax.axis_size("grp")
    here = lax.axis_index("grp")
    store_vals = jnp.zeros((n_groups,) + group_vals.shape, jnp.float32)
    store_labels = jnp.zeros((n_groups,) + group_labels.shape, jnp.float32)
    store_vals = lax.dynamic_update_index_in_dim(store_vals, group_vals, here, 0)
    store_labels = lax.dynamic_update_index_in_dim(store_labels, group_labels, here, 0)

    def advance(rounds, carry):
        moving_vals, moving_labels, kept_vals, kept_labels = carry
        moving_vals, moving_labels = from_behind((moving_vals, moving_labels), "grp", 1)
        source = (here - rounds) % n_groups
        kept_vals = lax.dynamic_update_index_in_dim(kept_vals, moving_vals, source, 0)
        kept_labels = lax.dynamic_update_index_in_dim(kept_labels, moving_labels, source, 0)
        return (moving_vals, moving_labels, kept_vals, kept_labels)

    carried = lax.fori_loop(
        1, n_groups, advance, (group_vals, group_labels, store_vals, store_labels)
    )
    all_vals = carried[2].reshape(-1, 128)
    all_labels = carried[3].reshape(-1).astype(jnp.int32)
    spread = (
        jnp.zeros((n_blocks, 128), jnp.float32).at[all_labels].add(all_vals).reshape(columns, width)
    )
    total = lax.dynamic_slice_in_dim(spread, lax.axis_index("dev") * part_width, part_width, 1)
    momentum_out = momentum_decay * momentum_in + total
    return (kept, momentum_out)


def solution(mesh):
    placed = (
        P(("grp", "dev"), None),
        P(("grp", "dev"), None),
        P(("grp", "dev"), None, None),
        P(("grp", "dev"), None),
        P(("grp", "dev")),
        P(None, "dev"),
    )
    return jax.shard_map(
        local,
        mesh=mesh,
        in_specs=placed,
        out_specs=(P(("grp", "dev"), None, None), P(None, "dev")),
        check_vma=False,
    )
```

profile of v0, /device:TPU:0, one launch (start us, length us, event | category | flops | bytes accessed | tf_op | source)
XLA Modules:
  0.0 100.5 jit_solution(11768598687038377532)
XLA Ops:
  0.7 0.7 copy-done
  1.4 4.9 %convolution_add_fusion = f32[64,12288]{1,0:T(8,128)S(1)} fusion(bf16[256,64]{0,1:T(8,128)(2,1)S(1)} %copy-done, bf16[256,12288]{1,0:T(8,128)(2,1)} %param.8, f32[1,64,12288]{2,1,0:T(8,128)} %param.10), kind=kOutput, calls=%fused_computation.4 | convolution fusion | flops 403439616 | bytes 12615680 | tf_op jit(solution)/shard_map/dot_general | solution.py:21
  6.3 1.9 %reshape.79 = f32[6144,128]{1,0:T(8,128)} reshape(f32[64,12288]{1,0:T(8,128)S(1)} %convolution_add_fusion) | data formatting | bytes 6291456 | tf_op jit(solution)/shard_map/reshape | solution.py:25
  8.3 2.5 %gather_fusion = f32[64,128]{1,0:T(8,128)S(1)} fusion(f32[6144,128]{1,0:T(8,128)} %reshape.79, s32[1024]{0:T(1024)S(1)} %pad_clamp_fusion), kind=kCustom, calls=%fused_computation | custom fusion | bytes 65792 | tf_op jit(solution)/shard_map/gather | solution.py:28
  11.5 15.9 %all_gather.6 = f32[512,128]{1,0:T(8,128)S(1)} all-gather(f32[64,128]{1,0:T(8,128)S(1)} %broadcast_multiply_fusion), channel_id=1, replica_groups=mesh['grp'=4,'dev'=8] {'dev'}, dimensions={0}, use_global_device_ids=true | all-gather | bytes 294912 | tf_op jit(solution)/shard_map/all_gather | solution.py:33
  27.5 0.6 copy-done.1
  28.1 1.0 copy-done.2
  29.1 0.6 dynamic-slice
  30.4 0.1 bitcast_dynamic-update-slice_fusion.2
  30.5 16.9 %all-reduce = f32[512]{0:T(512)S(1)} all-reduce(f32[512]{0:T(512)S(1)} %bitcast_dynamic-update-slice_fusion.2), channel_id=2, replica_groups=mesh['grp'=4,'dev'=8] {'dev'}, use_global_device_ids=true, to_apply=%add | all-reduce | flops 512 | bytes 4096 | tf_op jit(solution)/shard_map/all_gather | solution.py:34
  47.4 27.6 %while.21 = (s32[]{:T(128)}, f32[512,128]{1,0:T(8,128)}, f32[512]{0:T(512)S(1)}, f32[4,512,128]{2,1,0:T(8,128)}, f32[4,512]{1,0:T(4,128)S(1)}, /*index=5*/s32[]{:T(128)}, s32[]{:T(128)}, s32[]{:T(128)}, s32[]{:T(128)}, s32[]{:T(128)}) while((s32[]{:T(128)}, f32[512,128]{1,0:T(8,128)}, f32[512]{0:T(512)S(1)}, f32[4,512,128]{2,1,0:T(8,128)}, ...), condition=%wide.region_2.3_spmd, body=%wide.region_1.2_spmd.sunk | while | flops 17 | bytes 2113880 | solution.py:51
  47.4 1.5 %collective-permute-start = (f32[512,128]{1,0:T(8,128)}, f32[512,128]{1,0:T(8,128)S(1)}, u32[]{:S(2)}, u32[]{:S(2)}) collective-permute-start(f32[512,128]{1,0:T(8,128)} %get-tuple-element.220), channel_id=1, source_target_pairs={{24,0},{0,8},{8,16},{16,24},{25,1},{1,9},{9,17},{17,25},{26,2},{2,... | collective-permute-start | bytes 786440 | tf_op jit(solution)/shard_map/while/body/eval_jaxpr/ppermute | solution.py:12
  49.0 1.5 %collective-permute-start.1 = (f32[512]{0:T(512)S(1)}, f32[512]{0:T(512)S(1)}, u32[]{:S(2)}, u32[]{:S(2)}) collective-permute-start(f32[512]{0:T(512)S(1)} %get-tuple-element.221), channel_id=1, source_target_pairs={{24,0},{0,8},{8,16},{16,24},{25,1},{1,9},{9,17},{17,25},{26,2},{2,... | collective-permute-start | bytes 6152 | tf_op jit(solution)/shard_map/while/body/eval_jaxpr/ppermute | solution.py:12
  50.5 4.5 %collective-permute-done.1 = f32[512]{0:T(512)S(1)} collective-permute-done((f32[512]{0:T(512)S(1)}, f32[512]{0:T(512)S(1)}, u32[]{:S(2)}, u32[]{:S(2)}) %collective-permute-start.1) | collective-permute-done | bytes 2080 | tf_op jit(solution)/shard_map/while/body/eval_jaxpr/ppermute | solution.py:12
  55.1 0.7 copy.27
  55.8 0.7 bitcast_dynamic-update-slice_fusion.4
  56.5 0.9 collective-permute-start
  57.4 2.0 %collective-permute-start.1 = (f32[512]{0:T(512)S(1)}, f32[512]{0:T(512)S(1)}, u32[]{:S(2)}, u32[]{:S(2)}) collective-permute-start(f32[512]{0:T(512)S(1)} %get-tuple-element.221), channel_id=1, source_target_pairs={{24,0},{0,8},{8,16},{16,24},{25,1},{1,9},{9,17},{17,25},{26,2},{2,... | collective-permute-start | bytes 6152 | tf_op jit(solution)/shard_map/while/body/eval_jaxpr/ppermute | solution.py:12
  59.5 5.1 %collective-permute-done.1 = f32[512]{0:T(512)S(1)} collective-permute-done((f32[512]{0:T(512)S(1)}, f32[512]{0:T(512)S(1)}, u32[]{:S(2)}, u32[]{:S(2)}) %collective-permute-start.1) | collective-permute-done | bytes 2080 | tf_op jit(solution)/shard_map/while/body/eval_jaxpr/ppermute | solution.py:12
  64.6 0.7 copy.27
  65.3 0.7 bitcast_dynamic-update-slice_fusion.4
  66.1 0.7 collective-permute-start
  66.7 2.3 %collective-permute-start.1 = (f32[512]{0:T(512)S(1)}, f32[512]{0:T(512)S(1)}, u32[]{:S(2)}, u32[]{:S(2)}) collective-permute-start(f32[512]{0:T(512)S(1)} %get-tuple-element.221), channel_id=1, source_target_pairs={{24,0},{0,8},{8,16},{16,24},{25,1},{1,9},{9,17},{17,25},{26,2},{2,... | collective-permute-start | bytes 6152 | tf_op jit(solution)/shard_map/while/body/eval_jaxpr/ppermute | solution.py:12
  69.0 4.5 %collective-permute-done.1 = f32[512]{0:T(512)S(1)} collective-permute-done((f32[512]{0:T(512)S(1)}, f32[512]{0:T(512)S(1)}, u32[]{:S(2)}, u32[]{:S(2)}) %collective-permute-start.1) | collective-permute-done | bytes 2080 | tf_op jit(solution)/shard_map/while/body/eval_jaxpr/ppermute | solution.py:12
  73.6 0.7 copy.27
  74.3 0.7 bitcast_dynamic-update-slice_fusion.4
  75.1 13.6 %scatter_custom_fusion.1 = f32[6144,128]{1,0:T(8,128)} fusion(s32[2048]{0:T(1024)S(1)} %bitcast.41, f32[2048,128]{1,0:T(8,128)} %bitcast.38, f32[]{:T(128)} %constant.79.clone.1), kind=kCustom, calls=%fused_computation.7 | custom fusion | flops 262144 | bytes 3146240 | tf_op jit(solution)/shard_map/scatter-add | solution.py:57
  88.7 4.3 %reshape.81 = f32[64,12288]{1,0:T(8,128)} reshape(f32[6144,128]{1,0:T(8,128)} %scatter_custom_fusion.1) | data formatting | bytes 6291456 | tf_op jit(solution)/shard_map/reshape | solution.py:57
  93.0 1.9 %dynamic-slice_add_fusion = f32[64,1536]{1,0:T(8,128)} fusion(f32[64,12288]{1,0:T(8,128)} %reshape.81, s32[]{:T(128)S(6)} %select_n.64, f32[64,1536]{1,0:T(8,128)} %param.13), kind=kLoop, calls=%fused_computation.9 | loop fusion | flops 196608 | bytes 1179652 | tf_op jit(solution)/shard_map/add | solution.py:60
  94.9 0.9 scatter_custom_fusion
  96.0 0.9 mul.34
  96.8 3.6 %fusion = f32[1,64,12288]{2,1,0:T(8,128)} fusion(f32[64,12288]{1,0:T(8,128)S(1)} %convolution_add_fusion, f32[8,8,96,128]{3,2,1,0:T(8,128)S(1)} %bitcast.37), kind=kLoop, calls=%fused_computation.6 | loop fusion | flops 786432 | bytes 9437184 | tf_op jit(solution)/shard_map/mul | solution.py:30
  (30 shorter events, 0.5 us)
Async XLA Ops:
  0.6 0.8 copy-start
  6.3 1.9 %copy-start.3 = (s32[1,64]{1,0:T(1,128)S(1)}, s32[1,64]{1,0:T(1,128)}, u32[]{:S(2)}) copy-start(s32[1,64]{1,0:T(1,128)} %param.11) | copy-start | bytes 772
  6.3 22.8 %copy-start.4 = (u32[32]{0:T(128)S(1)}, u32[32]{0:T(128)}, u32[]{:S(2)}) copy-start(u32[32]{0:T(128)} %constant.93) | copy-start | bytes 388
  27.4 0.7 copy-start.1
  28.1 1.0 copy-start.2
  47.4 7.6 %collective-permute-start = (f32[512,128]{1,0:T(8,128)}, f32[512,128]{1,0:T(8,128)S(1)}, u32[]{:S(2)}, u32[]{:S(2)}) collective-permute-start(f32[512,128]{1,0:T(8,128)} %get-tuple-element.220), channel_id=1, source_target_pairs={{24,0},{0,8},{8,16},{16,24},{25,1},{1,9},{9,17},{17,25},{26,2},{2,... | collective-permute-start | bytes 786440 | tf_op jit(solution)/shard_map/while/body/eval_jaxpr/ppermute | solution.py:12
  49.0 6.0 %collective-permute-start.1 = (f32[512]{0:T(512)S(1)}, f32[512]{0:T(512)S(1)}, u32[]{:S(2)}, u32[]{:S(2)}) collective-permute-start(f32[512]{0:T(512)S(1)} %get-tuple-element.221), channel_id=1, source_target_pairs={{24,0},{0,8},{8,16},{16,24},{25,1},{1,9},{9,17},{17,25},{26,2},{2,... | collective-permute-start | bytes 6152 | tf_op jit(solution)/shard_map/while/body/eval_jaxpr/ppermute | solution.py:12
  56.5 8.1 %collective-permute-start = (f32[512,128]{1,0:T(8,128)}, f32[512,128]{1,0:T(8,128)S(1)}, u32[]{:S(2)}, u32[]{:S(2)}) collective-permute-start(f32[512,128]{1,0:T(8,128)} %get-tuple-element.220), channel_id=1, source_target_pairs={{24,0},{0,8},{8,16},{16,24},{25,1},{1,9},{9,17},{17,25},{26,2},{2,... | collective-permute-start | bytes 786440 | tf_op jit(solution)/shard_map/while/body/eval_jaxpr/ppermute | solution.py:12
  57.4 7.2 %collective-permute-start.1 = (f32[512]{0:T(512)S(1)}, f32[512]{0:T(512)S(1)}, u32[]{:S(2)}, u32[]{:S(2)}) collective-permute-start(f32[512]{0:T(512)S(1)} %get-tuple-element.221), channel_id=1, source_target_pairs={{24,0},{0,8},{8,16},{16,24},{25,1},{1,9},{9,17},{17,25},{26,2},{2,... | collective-permute-start | bytes 6152 | tf_op jit(solution)/shard_map/while/body/eval_jaxpr/ppermute | solution.py:12
  66.1 7.6 %collective-permute-start = (f32[512,128]{1,0:T(8,128)}, f32[512,128]{1,0:T(8,128)S(1)}, u32[]{:S(2)}, u32[]{:S(2)}) collective-permute-start(f32[512,128]{1,0:T(8,128)} %get-tuple-element.220), channel_id=1, source_target_pairs={{24,0},{0,8},{8,16},{16,24},{25,1},{1,9},{9,17},{17,25},{26,2},{2,... | collective-permute-start | bytes 786440 | tf_op jit(solution)/shard_map/while/body/eval_jaxpr/ppermute | solution.py:12
  66.7 6.8 %collective-permute-start.1 = (f32[512]{0:T(512)S(1)}, f32[512]{0:T(512)S(1)}, u32[]{:S(2)}, u32[]{:S(2)}) collective-permute-start(f32[512]{0:T(512)S(1)} %get-tuple-element.221), channel_id=1, source_target_pairs={{24,0},{0,8},{8,16},{16,24},{25,1},{1,9},{9,17},{17,25},{26,2},{2,... | collective-permute-start | bytes 6152 | tf_op jit(solution)/shard_map/while/body/eval_jaxpr/ppermute | solution.py:12
where the time goes:
time: 101 us; the launch traced here: 100 us
  blocking collectives  32.8 us (32%)
  other arithmetic  20.3 us (20%)
  local copies, waits for them, and re-layouts  17.1 us (17%)
  waiting for transfers between devices  14.2 us (14%)
  starting transfers between devices  8.97 us (9%)
  matrix products  4.91 us (5%)
  between operations  2.04 us (2%)
    all_gather x1, blocking collectives, local(): lax.all_gather(labels, 'dev', axis=0, tiled=True)  16.9 us
    all_gather x1, blocking collectives, local(): lax.all_gather(picked, 'dev', axis=0, tiled=True)  15.9 us
    ppermute x6, waiting for transfers between devices, from_behind(): return lax.ppermute(block, axis, route)  14.2 us
    scatter-add x1, other arithmetic, local(): jnp.zeros((n_blocks, 128), jnp.float32).at[all_labels].add(all_vals)  13.6 us
    ppermute x6, starting transfers between devices, from_behind(): return lax.ppermute(block, axis, route)  8.97 us
    dot_general x1, matrix products, local(): lax.dot_general(grads_out, acts, (((0,), (0,)), ((), ())), preferred_elem...  4.91 us
    reshape x1, local copies, waits for them, and re-layouts, local(): jnp.zeros((n_blocks, 128), jnp.float32).at[all_labels].add(all_vals)  4.3 us
    mul x1, other arithmetic, local(): kept = (blocks * (1.0 - marked)[:, None]).reshape(1, columns, width)  3.64 us
  transfers between devices with their start and end apart: 6, of which 3 were waited for; matrix products, arithmetic and copies ran while one was open for 0% of the time, Pallas kernels for 0%

commit v1 on v0

--- a/solution.py
+++ b/solution.py
@@ -29,9 +29,18 @@
     marked = jnp.zeros((n_blocks,), jnp.float32).at[chosen].max(valid_rows)
     kept = (blocks * (1.0 - marked)[:, None]).reshape(1, columns, width)
     labels = chosen.astype(jnp.float32)
+    choose_region = lambda view, lane_axis: jnp.concatenate(
+        lax.all_to_all(
+            jnp.stack([view for _ in range(lax.psum(1, axis_name=lane_axis))], axis=0),
+            axis_name=lane_axis,
+            split_axis=0,
+            concat_axis=0,
+        ),
+        axis=0,
+    )
     group_vals, group_labels = (
         lax.all_gather(picked, "dev", axis=0, tiled=True),
-        lax.all_gather(labels, "dev", axis=0, tiled=True),
+        choose_region(labels, "dev"),
     )
     n_groups = lax.axis_size("grp")
     here = lax.axis_index("grp")

time: 101 us -> 85 us (0.84)
  blocking collectives: 32.8 us -> 14.7 us
  local copies, waits for them, and re-layouts: 17.1 us -> 9.91 us
  starting transfers between devices: 8.97 us -> 15.4 us
  waiting for transfers between devices: 14.2 us -> 17 us
    all_gather x1 -> x0, blocking collectives: 16.9 us -> none  [local(): lax.all_gather(labels, 'dev', axis=0, tiled=True)]
    all_to_all x0 -> x1, starting transfers between devices: none -> 6.35 us  [local(): lax.all_to_all(jnp.stack([view for _ in range(lax.psum(1, axis_name=lane_...]
    ppermute x6, waiting for transfers between devices: 14.2 us -> 17 us  [from_behind(): return lax.ppermute(block, axis, route)]
    reshape x1, local copies, waits for them, and re-layouts: 4.3 us -> 1.97 us  [local(): jnp.zeros((n_blocks, 128), jnp.float32).at[all_labels].add(all_vals)]
    dynamic_update_slice x3, local copies, waits for them, and re-layouts: 2.16 us -> 0.07 us  [advance(): lax.dynamic_update_index_in_dim(kept_vals, moving_vals, source, 0)]
    while x6, local copies, waits for them, and re-layouts: 2.12 us -> 0.06 us
    unnamed x13 -> x5, local copies, waits for them, and re-layouts: 2.97 us -> 0.95 us
    all_gather x1, blocking collectives: 15.9 us -> 14.7 us  [local(): lax.all_gather(picked, 'dev', axis=0, tiled=True)]
  transfers between devices with their start and end apart: 6 -> 7, of which waited for: 3 -> 3; matrix products, arithmetic and copies ran while one was open for 0% -> 19% of each run, Pallas kernels for 0% -> 0%
where the time goes in v1:
time: 85 us; the launch traced here: 84.7 us
  other arithmetic  21.1 us (25%)
  waiting for transfers between devices  17 us (20%)
  starting transfers between devices  15.4 us (18%)
  blocking collectives  14.7 us (17%)
  local copies, waits for them, and re-layouts  9.91 us (12%)
  matrix products  4.91 us (6%)
  between operations  1.41 us (2%)
    ppermute x6, waiting for transfers between devices, from_behind(): return lax.ppermute(block, axis, route)  17 us
    all_gather x1, blocking collectives, local(): lax.all_gather(picked, 'dev', axis=0, tiled=True)  14.7 us
    scatter-add x1, other arithmetic, local(): jnp.zeros((n_blocks, 128), jnp.float32).at[all_labels].add(all_vals)  12.6 us
    ppermute x6, starting transfers between devices, from_behind(): return lax.ppermute(block, axis, route)  9.09 us
    all_to_all x1, starting transfers between devices, local(): lax.all_to_all(jnp.stack([view for _ in range(lax.psum(1, axis_name=lane_...  6.35 us
    dot_general x1, matrix products, local(): lax.dot_general(grads_out, acts, (((0,), (0,)), ((), ())), preferred_elem...  4.91 us
    mul x1, other arithmetic, local(): kept = (blocks * (1.0 - marked)[:, None]).reshape(1, columns, width)  3.64 us
    gather x1, local copies, waits for them, and re-layouts, local(): picked = blocks[chosen] * valid_rows[:, None]  2.49 us
  transfers between devices with their start and end apart: 7, of which 3 were waited for; matrix products, arithmetic and copies ran while one was open for 19% of the time, Pallas kernels for 0%

profile of v1, /device:TPU:0, one launch (start us, length us, event | category | flops | bytes accessed | tf_op | source)
XLA Modules:
  0.0 84.7 jit_solution(4638347930431029947)
XLA Ops:
  0.6 0.7 convert_bitcast_fusion.1
  1.3 0.6 stack.2
  1.9 6.4 %all-to-all-start = ((f32[8,1,64]{2,1,0:T(1,128)}), f32[8,1,64]{2,1,0:T(1,128)S(1)}, u32[]{:S(2)}, u32[]{:S(2)}) async-start(f32[8,1,64]{2,1,0:T(1,128)} %stack.2), calls=%async_computation | async-start | bytes 8192 | tf_op jit(solution)/shard_map/all_to_all | solution.py:33
  8.3 0.7 fusion.5
  8.9 4.9 %convolution_add_fusion = f32[64,12288]{1,0:T(8,128)S(1)} fusion(bf16[256,64]{0,1:T(8,128)(2,1)S(1)} %copy-done, bf16[256,12288]{1,0:T(8,128)(2,1)} %param.8, f32[1,64,12288]{2,1,0:T(8,128)} %param.10), kind=kOutput, calls=%fused_computation.4 | convolution fusion | flops 403439616 | bytes 12615680 | tf_op jit(solution)/shard_map/dot_general | solution.py:21
  13.8 1.9 %reshape.91 = f32[6144,128]{1,0:T(8,128)} reshape(f32[64,12288]{1,0:T(8,128)S(1)} %convolution_add_fusion) | data formatting | bytes 6291456 | tf_op jit(solution)/shard_map/reshape | solution.py:25
  16.4 2.5 %gather_fusion = f32[64,128]{1,0:T(8,128)S(1)} fusion(f32[6144,128]{1,0:T(8,128)} %reshape.91, s32[1024]{0:T(1024)S(1)} %pad_clamp_fusion), kind=kCustom, calls=%fused_computation | custom fusion | bytes 65792 | tf_op jit(solution)/shard_map/gather | solution.py:28
  18.9 0.1 broadcast_multiply_fusion
  19.0 14.7 %all_gather.3 = f32[512,128]{1,0:T(8,128)S(1)} all-gather(f32[64,128]{1,0:T(8,128)S(1)} %broadcast_multiply_fusion), channel_id=1, replica_groups=mesh['grp'=4,'dev'=8] {'dev'}, dimensions={0}, use_global_device_ids=true | all-gather | bytes 294912 | tf_op jit(solution)/shard_map/all_gather | solution.py:42
  33.7 0.9 %scatter_custom_fusion = f32[6144]{0:T(1024)S(1)} fusion(s32[64]{0:T(128)S(1)} %fusion.5, f32[64]{0:T(128)S(1)} %compare_convert_fusion, f32[]{:T(128)} %constant.79.clone.1), kind=kCustom, calls=%fused_computation.13 | custom fusion | flops 64 | bytes 24580 | tf_op jit(solution)/shard_map/scatter-max | solution.py:29
  34.7 0.1 mul.33
  34.7 0.9 %mul.34 = f32[64,96,128]{2,1,0:T(8,128)S(1)} broadcast(f32[64,96]{1,0:T(8,128)S(1)} %mul.33), dimensions={0,1} | broadcast | bytes 3170304 | tf_op jit(solution)/shard_map/mul | solution.py:30
  35.6 3.6 %fusion = f32[1,64,12288]{2,1,0:T(8,128)} fusion(f32[64,12288]{1,0:T(8,128)S(1)} %convolution_add_fusion, f32[8,8,96,128]{3,2,1,0:T(8,128)S(1)} %bitcast.36), kind=kLoop, calls=%fused_computation.6 | loop fusion | flops 786432 | bytes 9437184 | tf_op jit(solution)/shard_map/mul | solution.py:30
  39.3 0.1 broadcast_in_dim.47
  39.4 0.1 broadcast_in_dim.50
  39.5 0.5 broadcast.60
  40.0 0.7 reduce.5
  40.6 0.1 reshape.92
  40.8 26.5 %while.21 = (s32[]{:T(128)}, f32[512,128]{1,0:T(8,128)S(1)}, f32[512]{0:T(512)S(1)}, f32[4,512,128]{2,1,0:T(8,128)S(1)}, f32[4,512]{1,0:T(4,128)S(1)}, /*index=5...) while((s32[]{:T(128)}, f32[512,128]{1,0:T(8,128)S(1)}, f32[512]{0:T(512)S(1)}, ...), condition=%wide.region_2.3_spmd, body=%wide.region_1.2_spmd.sunk | while | flops 17 | bytes 2113880 | solution.py:60
  40.8 1.5 %collective-permute-start = (f32[512,128]{1,0:T(8,128)S(1)}, f32[512,128]{1,0:T(8,128)S(1)}, u32[]{:S(2)}, u32[]{:S(2)}) collective-permute-start(f32[512,128]{1,0:T(8,128)S(1)} %get-tuple-element.220), channel_id=1, source_target_pairs={{24,0},{0,8},{8,16},{16,24},{25,1},{1,9},{9,17},{17,25},{26,2},{2,... | collective-permute-start | bytes 786440 | tf_op jit(solution)/shard_map/while/body/eval_jaxpr/ppermute | solution.py:12
  42.3 1.5 %collective-permute-start.1 = (f32[512]{0:T(512)S(1)}, f32[512]{0:T(512)S(1)}, u32[]{:S(2)}, u32[]{:S(2)}) collective-permute-start(f32[512]{0:T(512)S(1)} %get-tuple-element.221), channel_id=1, source_target_pairs={{24,0},{0,8},{8,16},{16,24},{25,1},{1,9},{9,17},{17,25},{26,2},{2,... | collective-permute-start | bytes 6152 | tf_op jit(solution)/shard_map/while/body/eval_jaxpr/ppermute | solution.py:12
  43.8 6.5 %collective-permute-done.1 = f32[512]{0:T(512)S(1)} collective-permute-done((f32[512]{0:T(512)S(1)}, f32[512]{0:T(512)S(1)}, u32[]{:S(2)}, u32[]{:S(2)}) %collective-permute-start.1) | collective-permute-done | bytes 2080 | tf_op jit(solution)/shard_map/while/body/eval_jaxpr/ppermute | solution.py:12
  50.4 0.6 collective-permute-start
  51.1 2.4 %collective-permute-start.1 = (f32[512]{0:T(512)S(1)}, f32[512]{0:T(512)S(1)}, u32[]{:S(2)}, u32[]{:S(2)}) collective-permute-start(f32[512]{0:T(512)S(1)} %get-tuple-element.221), channel_id=1, source_target_pairs={{24,0},{0,8},{8,16},{16,24},{25,1},{1,9},{9,17},{17,25},{26,2},{2,... | collective-permute-start | bytes 6152 | tf_op jit(solution)/shard_map/while/body/eval_jaxpr/ppermute | solution.py:12
  53.5 5.7 %collective-permute-done.1 = f32[512]{0:T(512)S(1)} collective-permute-done((f32[512]{0:T(512)S(1)}, f32[512]{0:T(512)S(1)}, u32[]{:S(2)}, u32[]{:S(2)}) %collective-permute-start.1) | collective-permute-done | bytes 2080 | tf_op jit(solution)/shard_map/while/body/eval_jaxpr/ppermute | solution.py:12
  59.3 0.1 collective-permute-start
  59.3 3.0 %collective-permute-start.1 = (f32[512]{0:T(512)S(1)}, f32[512]{0:T(512)S(1)}, u32[]{:S(2)}, u32[]{:S(2)}) collective-permute-start(f32[512]{0:T(512)S(1)} %get-tuple-element.221), channel_id=1, source_target_pairs={{24,0},{0,8},{8,16},{16,24},{25,1},{1,9},{9,17},{17,25},{26,2},{2,... | collective-permute-start | bytes 6152 | tf_op jit(solution)/shard_map/while/body/eval_jaxpr/ppermute | solution.py:12
  62.3 4.8 %collective-permute-done.1 = f32[512]{0:T(512)S(1)} collective-permute-done((f32[512]{0:T(512)S(1)}, f32[512]{0:T(512)S(1)}, u32[]{:S(2)}, u32[]{:S(2)}) %collective-permute-start.1) | collective-permute-done | bytes 2080 | tf_op jit(solution)/shard_map/while/body/eval_jaxpr/ppermute | solution.py:12
  67.3 0.9 %copy-done.1 = f32[4,512,128]{2,1,0:T(8,128)} copy-done((f32[4,512,128]{2,1,0:T(8,128)}, f32[4,512,128]{2,1,0:T(8,128)S(1)}, u32[]{:S(2)}) %copy-start.1) | copy-done | bytes 1048600
  68.2 12.6 %scatter_custom_fusion.1 = f32[6144,128]{1,0:T(8,128)S(1)} fusion(s32[2048]{0:T(1024)S(1)} %bitcast.41, f32[2048,128]{1,0:T(8,128)} %bitcast.37, f32[]{:T(128)} %constant.79.clone.1), kind=kCustom, calls=%fused_computation.7 | custom fusion | flops 262144 | bytes 3146240 | tf_op jit(solution)/shard_map/scatter-add | solution.py:66
  80.8 2.0 %reshape.94 = f32[64,12288]{1,0:T(8,128)} reshape(f32[6144,128]{1,0:T(8,128)S(1)} %scatter_custom_fusion.1) | data formatting | bytes 6291456 | tf_op jit(solution)/shard_map/reshape | solution.py:66
  82.8 1.9 %dynamic-slice_add_fusion = f32[64,1536]{1,0:T(8,128)} fusion(f32[64,12288]{1,0:T(8,128)} %reshape.94, s32[]{:T(128)S(6)} %select_n.64, f32[64,1536]{1,0:T(8,128)} %param.13), kind=kLoop, calls=%fused_computation.9 | loop fusion | flops 196608 | bytes 1179652 | tf_op jit(solution)/shard_map/add | solution.py:69
  (28 shorter events, 0.4 us)
Async XLA Ops:
  0.6 8.3 %copy-start = (bf16[256,64]{0,1:T(8,128)(2,1)S(1)}, bf16[256,64]{0,1:T(8,128)(2,1)}, u32[]{:S(2)}) copy-start(bf16[256,64]{0,1:T(8,128)(2,1)} %param.9) | copy-start | bytes 98308
  1.9 37.5 %all-to-all-start = ((f32[8,1,64]{2,1,0:T(1,128)}), f32[8,1,64]{2,1,0:T(1,128)S(1)}, u32[]{:S(2)}, u32[]{:S(2)}) async-start(f32[8,1,64]{2,1,0:T(1,128)} %stack.2), calls=%async_computation | async-start | bytes 8192 | tf_op jit(solution)/shard_map/all_to_all | solution.py:33
  40.8 9.6 %collective-permute-start = (f32[512,128]{1,0:T(8,128)S(1)}, f32[512,128]{1,0:T(8,128)S(1)}, u32[]{:S(2)}, u32[]{:S(2)}) collective-permute-start(f32[512,128]{1,0:T(8,128)S(1)} %get-tuple-element.220), channel_id=1, source_target_pairs={{24,0},{0,8},{8,16},{16,24},{25,1},{1,9},{9,17},{17,25},{26,2},{2,... | collective-permute-start | bytes 786440 | tf_op jit(solution)/shard_map/while/body/eval_jaxpr/ppermute | solution.py:12
  42.3 8.0 %collective-permute-start.1 = (f32[512]{0:T(512)S(1)}, f32[512]{0:T(512)S(1)}, u32[]{:S(2)}, u32[]{:S(2)}) collective-permute-start(f32[512]{0:T(512)S(1)} %get-tuple-element.221), channel_id=1, source_target_pairs={{24,0},{0,8},{8,16},{16,24},{25,1},{1,9},{9,17},{17,25},{26,2},{2,... | collective-permute-start | bytes 6152 | tf_op jit(solution)/shard_map/while/body/eval_jaxpr/ppermute | solution.py:12
  50.4 8.7 %collective-permute-start = (f32[512,128]{1,0:T(8,128)S(1)}, f32[512,128]{1,0:T(8,128)S(1)}, u32[]{:S(2)}, u32[]{:S(2)}) collective-permute-start(f32[512,128]{1,0:T(8,128)S(1)} %get-tuple-element.220), channel_id=1, source_target_pairs={{24,0},{0,8},{8,16},{16,24},{25,1},{1,9},{9,17},{17,25},{26,2},{2,... | collective-permute-start | bytes 786440 | tf_op jit(solution)/shard_map/while/body/eval_jaxpr/ppermute | solution.py:12
  51.1 8.1 %collective-permute-start.1 = (f32[512]{0:T(512)S(1)}, f32[512]{0:T(512)S(1)}, u32[]{:S(2)}, u32[]{:S(2)}) collective-permute-start(f32[512]{0:T(512)S(1)} %get-tuple-element.221), channel_id=1, source_target_pairs={{24,0},{0,8},{8,16},{16,24},{25,1},{1,9},{9,17},{17,25},{26,2},{2,... | collective-permute-start | bytes 6152 | tf_op jit(solution)/shard_map/while/body/eval_jaxpr/ppermute | solution.py:12
  59.3 7.9 %collective-permute-start = (f32[512,128]{1,0:T(8,128)S(1)}, f32[512,128]{1,0:T(8,128)S(1)}, u32[]{:S(2)}, u32[]{:S(2)}) collective-permute-start(f32[512,128]{1,0:T(8,128)S(1)} %get-tuple-element.220), channel_id=1, source_target_pairs={{24,0},{0,8},{8,16},{16,24},{25,1},{1,9},{9,17},{17,25},{26,2},{2,... | collective-permute-start | bytes 786440 | tf_op jit(solution)/shard_map/while/body/eval_jaxpr/ppermute | solution.py:12
  59.3 7.8 %collective-permute-start.1 = (f32[512]{0:T(512)S(1)}, f32[512]{0:T(512)S(1)}, u32[]{:S(2)}, u32[]{:S(2)}) collective-permute-start(f32[512]{0:T(512)S(1)} %get-tuple-element.221), channel_id=1, source_target_pairs={{24,0},{0,8},{8,16},{16,24},{25,1},{1,9},{9,17},{17,25},{26,2},{2,... | collective-permute-start | bytes 6152 | tf_op jit(solution)/shard_map/while/body/eval_jaxpr/ppermute | solution.py:12
  67.2 1.0 %copy-start.1 = (f32[4,512,128]{2,1,0:T(8,128)}, f32[4,512,128]{2,1,0:T(8,128)S(1)}, u32[]{:S(2)}) copy-start(f32[4,512,128]{2,1,0:T(8,128)S(1)} %get-tuple-element.159) | copy-start | bytes 3145732
